TPU v7x, 32 devices: a whole 2x2x4 slice. The times are simulated.
32 devices in a mesh: groups: 2 (over y), ga: 16 (over z, x, core).
Axes of the slice: x: 2, y: 2, z: 4, core: 2. Of those that a mesh axis runs over, the one named last changes fastest.
Arguments:
- occupied: float32 [2, 1024, 12288], P(None, None, 'ga'), may hold values from -0.0546875 to 0.0546875
- residual: float32 [4, 2, 128, 12288], P('groups', None, None, 'ga'), parts along dimension 0, may hold values from -6 to 6
- old_direction: float32 [4, 2, 128, 12288], P('groups', None, None, 'ga'), parts along dimension 0, may hold values from -6 to 6
- kin_ratio: float32 [12288], P('ga'), may hold values from 0.06 to 5, as said below
- old_dot: float32 [4, 128], P('groups'), parts along dimension 0, may hold values from 6144 to 24576
Outputs:
- direction: float32 [4, 2, 128, 12288], P('groups', None, None, 'ga'), parts along dimension 0
- dot_new: float32 [4, 128], P('groups'), parts along dimension 0
There are 2 independent parts, one for each index of `groups`. A program takes and returns all parts, laid end to end along the dimension named above; an argument that names none is the same for every part. Nothing has to cross between parts.
Inputs may be any that keep to these rules, and one draw needn't show every extreme that they name: `kin_ratio`: positive; grows with the plane-wave index on average and varies from one plane wave to the next.
All inputs are finite; a program needn't handle non-finite values.
Results may differ from a plain program's by a relative error of at most 0.000056.
Values sent between devices are 32-bit elements; how exact they have to be, the bound alone decides.
A program may use at most 64 MiB of HBM per device.

v0:
```python
import jax
import jax.numpy as jnp
from jax import lax
from jax.sharding import PartitionSpec as P

highest = lax.Precision.HIGHEST


def teter_factor(ratio):
    numerator = 27.0 + 18.0 * ratio + 12.0 * ratio**2 + 8.0 * ratio**3
    return numerator / (numerator + 16.0 * ratio**4)


def margins(occupied, vectors):
    products = jnp.einsum("hng,pcbg->phcnb", occupied, vectors, precision=highest)
    real_part = products[:, 0, 0] + products[:, 1, 1]
    imag_part = products[:, 0, 1] - products[:, 1, 0]
    return jnp.stack([real_part, imag_part], axis=1)


def correction(summed, occ_rows):
    real_part = summed[:, 0]
    imag_part = summed[:, 1]
    coefficient = jnp.stack(
        [jnp.stack([real_part, -imag_part], axis=1), jnp.stack([imag_part, real_part], axis=1)],
        axis=1,
    )
    return jnp.einsum("pchnb,hng->pcbg", coefficient, occ_rows, precision=highest)


def on_device(occupied, residual, old_direction, kin_ratio, old_dot):
    factor = teter_factor(kin_ratio)
    first = margins(occupied, residual)
    first_total = lax.psum(first, "ga")
    gradient = residual - correction(first_total, occupied)
    precond = factor * gradient
    local_dot = jnp.sum(factor * (gradient[:, 0] ** 2 + gradient[:, 1] ** 2), axis=-1)
    second = margins(occupied, precond)
    second_total, dot_new = lax.psum((second, local_dot), "ga")
    projected = precond - correction(second_total, occupied)
    direction = projected + (dot_new / old_dot)[:, None, :, None] * old_direction
    return (direction, dot_new)


def solution(mesh):
    placed = (
        P(None, None, "ga"),
        P("groups", None, None, "ga"),
        P("groups", None, None, "ga"),
        P("ga"),
        P("groups", None),
    )
    return jax.shard_map(
        on_device,
        mesh=mesh,
        in_specs=placed,
        out_specs=(P("groups", None, None, "ga"), P("groups", None)),
        check_vma=False,
    )
```

profile of v0, /device:TPU:0, one launch (start us, length us, event | category | flops | bytes accessed | tf_op | source)
XLA Modules:
  0.0 279.0 jit_solution(1500607859630223277)
XLA Ops:
  7.2 0.0 all-reduce.3.cloned.1.call-start
  7.2 13.1 %fusion.10 = f32[2,2,2,1024,128]{3,4,1,2,0:T(8,128)S(1)} fusion(f32[2,1024,768]{2,1,0:T(8,128)} %param.5, f32[2,2,128,768]{3,2,1,0:T(8,128)} %param.6), kind=kOutput, calls=%fused_computation.12 | convolution fusion | flops 9663676416 | bytes 12058624 | tf_op jit(solution)/shard_map/hng,pcbg->phcnb/dot_general | solution.py:15
  20.4 0.2 fusion.31
  20.5 0.2 fusion.33
  20.7 1.4 pad_maximum_fusion.2
  22.1 0.0 all-reduce.3.cloned.1.call-update
  22.2 0.2 all-reduce.5.cloned.1.call-start
  22.4 0.4 copy-done.3
  22.8 100.4 %all-reduce.3.cloned.1.call-done = f32[2,2,1024,128]{2,3,0,1:T(8,128)} async-done(((f32[2,2,1024,128]{2,3,0,1:T(8,128)}), f32[2,2,1024,128]{2,3,0,1:T(8,128)}) %all-reduce.3.cloned.1.call-update) | async-done | bytes 2097168 | tf_op jit(solution)/shard_map/psum | solution.py:34
  123.2 1.9 slice_negate_fusion.1
  125.2 0.5 maximum_bitcast_fusion
  125.7 0.9 copy-done
  126.6 16.2 %bitcast_subtract_fusion.1 = f32[2,2,128,768]{3,2,1,0:T(8,128)S(1)} fusion(f32[2,2,128,768]{3,2,1,0:T(8,128)S(1)} %copy-done, f32[2,1024,768]{2,1,0:T(8,128)} %param.5, f32[2,1,2,1024,128]{3,4,0,2,1:T(8,128)S(1)} %get-tuple-element.11, f32[2,1,2,1024,128]{3,4,0,2,1:T(8,128)S(1)} %get-tuple-element.10), kind=kOutput, calls=%fused_computation.24 | convolution fusion | flops 9665118208 | bytes 13631488 | tf_op jit(solution)/shard_map/pchnb,hng->pcbg/dot_general | solution.py:28
  142.8 10.2 %fusion.13 = f32[2,2,2,1024,128]{3,4,1,2,0:T(8,128)S(1)} fusion(f32[2,1024,768]{2,1,0:T(8,128)S(1)} %bitcast.84, f32[2,2,128,768]{3,2,1,0:T(8,128)S(1)} %bitcast_subtract_fusion.1, f32[768]{0:T(1024)S(1)} %add_divide_fusion), kind=kOutput, calls=%fused_computation.13 | convolution fusion | flops 9664069632 | bytes 12061696 | tf_op jit(solution)/shard_map/hng,pcbg->phcnb/dot_general | solution.py:15
  153.0 0.2 fusion.28
  153.1 0.2 fusion.30
  153.3 1.4 pad_maximum_fusion.3
  154.8 0.2 fusion.37
  155.0 31.1 %psum.23 = f32[2,128]{1,0:T(2,128)S(1)} all-reduce(f32[2,128]{1,0:T(2,128)S(1)} %fusion.37), channel_id=1, replica_groups=mesh['groups'=2,'ga'=16] {'ga'}, use_global_device_ids=true, to_apply=%region_3.0 | all-reduce | flops 256 | bytes 2048 | tf_op jit(solution)/shard_map/psum | solution.py:39
  186.1 66.3 %all-reduce.5.cloned.1.call-done = f32[2,2,1024,128]{2,3,0,1:T(8,128)} async-done(((f32[2,2,1024,128]{2,3,0,1:T(8,128)}), f32[2,2,1024,128]{2,3,0,1:T(8,128)}) %all-reduce.5.cloned.1.call-update) | async-done | bytes 2097168 | tf_op jit(solution)/shard_map/psum | solution.py:39
  252.5 1.9 slice_negate_fusion
  254.4 0.5 maximum_bitcast_fusion.2
  254.9 0.9 copy-done.1
  255.8 16.4 %fusion.18 = f32[2,2,128,768]{3,2,1,0:T(8,128)} fusion(f32[2,2,128,768]{3,2,1,0:T(8,128)S(1)} %copy-done.1, f32[2,1024,768]{2,1,0:T(8,128)} %param.5, f32[2,2,128,768]{3,2,1,0:T(8,128)S(1)} %bitcast_subtract_fusion.1, f32[2,128]{1,0:T(2,128)S(1)} %div.7, f32[768]{0:T(1024)S(1)} %add_divide_fusion, f32[2,1,2,1024,128]{3,4,0,2,1:T(8,128)S(1)} %get-tuple-element.9, ...), kind=kOutput, calls=%fused_computation.23 | convolution fusion | flops 9666297856 | bytes 15208448 | tf_op jit(solution)/shard_map/pchnb,hng->pcbg/dot_general | solution.py:28
  (15 shorter events, 0.1 us)
Async XLA Ops:
  7.2 116.1 %all-reduce.3.cloned.1.call-start = ((), (), s32[]{:S(2)}) async-start(), calls=%async_computation | async-start | bytes 4194304 | tf_op jit(solution)/shard_map/psum | solution.py:34
  22.1 0.7 copy-start.3
  22.2 230.3 %all-reduce.5.cloned.1.call-start = ((), (), s32[]{:S(2)}) async-start(), calls=%async_computation.1 | async-start | bytes 4194304 | tf_op jit(solution)/shard_map/psum | solution.py:39
  125.1 1.4 copy-start
  125.1 17.6 %slice-start = ((s8[6291456]{0:T(1024)(128)(4,1)}), s8[4194304]{0:T(1024)(128)(4,1)S(1)}, s32[]{:S(2)}) async-start(s8[6291456]{0:T(1024)(128)(4,1)} %bitcast.83), calls=%async_computation.2 | async-start | bytes 8388608
  126.5 16.2 %slice-start.1 = ((s8[6291456]{0:T(1024)(128)(4,1)}), s8[2097152]{0:T(1024)(128)(4,1)S(1)}, s32[]{:S(2)}) async-start(s8[6291456]{0:T(1024)(128)(4,1)} %bitcast.83), calls=%async_computation.3 | async-start | bytes 4194304
  154.7 31.4 %copy-start.4 = (f32[2,128]{1,0:T(2,128)S(1)}, f32[2,128]{1,0:T(2,128)}, u32[]{:S(2)}) copy-start(f32[2,128]{1,0:T(2,128)} %param.9) | copy-start | bytes 3076
  186.1 68.3 %copy-start.2 = (f32[2,128]{1,0:T(2,128)}, f32[2,128]{1,0:T(2,128)S(1)}, u32[]{:S(2)}) copy-start(f32[2,128]{1,0:T(2,128)S(1)} %psum.23) | copy-start | bytes 3076
  254.4 1.4 copy-start.1
Sparse Core Ops, SparseCore 0:
  22.3 100.8 all-reduce.2
  154.9 97.5 all-reduce.4
where the time goes:
time: 279 us
  waiting for transfers between devices  167 us (60%)
  matrix products  55.9 us (20%)
  blocking collectives  31.1 us (11%)
  between operations  14.2 us (5%)
  other arithmetic  8.56 us (3%)
    psum x1, waiting for transfers between devices, on_device(): first_total = lax.psum(first, 'ga')  100 us
    psum x1, waiting for transfers between devices, on_device(): second_total, dot_new = lax.psum((second, local_dot), 'ga')  66.3 us
    dot_general x2, matrix products, correction(): jnp.einsum('pchnb,hng->pcbg', coefficient, occ_rows, precision=highest)  32.6 us
    psum x1, blocking collectives, on_device(): second_total, dot_new = lax.psum((second, local_dot), 'ga')  31.1 us
    dot_general x2, matrix products, margins(): jnp.einsum('hng,pcbg->phcnb', occupied, vectors, precision=highest)  23.3 us
  transfers between devices with their start and end apart: 2, of which 2 were waited for; matrix products, arithmetic and copies ran while one was open for 0% of the time, Pallas kernels for 0%

commit v1 on v0

v1 whole, which is shorter than its diff:
```python
import functools
import math

import jax
import jax.numpy as jnp
from jax import lax
from jax.experimental import pallas as pl
from jax.experimental.pallas import tpu as pltpu
from jax.sharding import PartitionSpec as P

HIGH = lax.Precision.HIGH


def teter_factor(ratio):
    numerator = 27.0 + 18.0 * ratio + 12.0 * ratio**2 + 8.0 * ratio**3
    return numerator / (numerator + 16.0 * ratio**4)


def levels_of(count):
    chips = count // 2
    inner = 2 ** (int(math.log2(chips)) // 2)
    return (2, inner, chips // inner)


def sum_kernel(levels, chunks, small, *refs):
    depth = len(levels)
    if small:
        x_ref, d_ref, o_ref, e_ref, *scratch = refs
        gathered = scratch[-depth:]
        scratch = scratch[:-depth]
    else:
        x_ref, o_ref, *scratch = refs
    recv = scratch[:depth]
    part = scratch[depth : 2 * depth - 1]
    send_sem, recv_sem = scratch[2 * depth - 1 :]
    me = lax.axis_index("ga")
    coords, strides, stride = [], [], 1
    for size in levels:
        coords.append((me // stride) % size)
        strides.append(stride)
        stride *= size
    rows = x_ref.shape[0] // chunks
    sizes = [rows]
    for size in levels:
        sizes.append(sizes[-1] // size)

    def peer(level, d):
        there = (coords[level] + d) % levels[level]
        return there, me + (there - coords[level]) * strides[level]

    barrier = pltpu.get_barrier_semaphore()
    total = 0
    for level in range(depth):
        for d in range(1, levels[level]):
            pl.semaphore_signal(barrier, inc=1, device_id={"ga": peer(level, d)[1]}, device_id_type=pl.DeviceIdType.MESH)
            total += 1
    pl.semaphore_wait(barrier, total)

    slot_of = {}

    def sem_slot(chunk, stage, d):
        return slot_of.setdefault((chunk, stage, d), len(slot_of))

    def own_start(chunk, level):
        start = chunk * rows
        for k in range(level):
            start = start + coords[k] * sizes[k + 1]
        return pl.multiple_of(start, 8)

    copies = {}

    def send(chunk, stage, d, src, dst, device):
        slot = sem_slot(chunk, stage, d)
        copy = pltpu.make_async_remote_copy(
            src_ref=src,
            dst_ref=dst,
            send_sem=send_sem.at[slot],
            recv_sem=recv_sem.at[slot],
            device_id={"ga": device},
            device_id_type=pl.DeviceIdType.MESH,
        )
        copy.start()
        copies[(chunk, stage, d)] = copy

    def source(chunk, level, which):
        height = sizes[level + 1]
        if level == 0:
            return x_ref.at[pl.ds(pl.multiple_of(chunk * rows + which * height, 8), height)]
        return part[level - 1].at[chunk, pl.ds(pl.multiple_of(which * height, 8), height)]

    def stage_run(chunk, stage):
        if 1 <= stage <= depth:
            level = stage - 1
            value = source(chunk, level, coords[level])[...]
            for d in range(1, levels[level]):
                copies[(chunk, stage - 1, d)].wait_recv()
                value = value + recv[level][chunk, d - 1]
            if level < depth - 1:
                part[level][chunk] = value
            else:
                o_ref[pl.ds(own_start(chunk, depth), sizes[depth])] = value
        elif stage > depth:
            level = 2 * depth - stage
            for d in range(1, levels[level]):
                copies[(chunk, stage - 1, d)].wait_recv()
        if stage < depth:
            for d in range(1, levels[stage]):
                there, device = peer(stage, d)
                send(chunk, stage, d, source(chunk, stage, there), recv[stage].at[chunk, d - 1], device)
        elif stage < 2 * depth:
            level = 2 * depth - 1 - stage
            block = o_ref.at[pl.ds(own_start(chunk, level + 1), sizes[level + 1])]
            for d in range(1, levels[level]):
                send(chunk, stage, d, block, block, peer(level, d)[1])

    def small_run(stage):
        if stage == 0:
            value = d_ref[...]
        else:
            for d in range(1, levels[stage - 1]):
                copies[("small", stage - 1, d)].wait_recv()
            value = gathered[stage - 1][0]
            for k in range(1, levels[stage - 1]):
                value = value + gathered[stage - 1][k]
        if stage == depth:
            e_ref[...] = value
            return
        gathered[stage][coords[stage]] = value
        block = gathered[stage].at[coords[stage]]
        for d in range(1, levels[stage]):
            send("small", stage, d, block, block, peer(stage, d)[1])

    for turn in range(chunks + 2 * depth):
        if small and turn <= depth:
            small_run(turn)
        for stage in reversed(range(2 * depth + 1)):
            chunk = turn - stage
            if 0 <= chunk < chunks:
                stage_run(chunk, stage)
    for copy in copies.values():
        copy.wait_send()


def sum_over_ga(x, count, ident, small=None):
    levels = levels_of(count)
    rows = x.shape[0]
    chunks = max(1, min(4, rows // (8 * count)))
    height = rows // chunks
    recv, part = [], []
    for level, size in enumerate(levels):
        height //= size
        recv.append(pltpu.VMEM((chunks, size - 1, height, x.shape[1]), x.dtype))
        if level < len(levels) - 1:
            part.append(pltpu.VMEM((chunks, height, x.shape[1]), x.dtype))
    slots = (2 * chunks + 1) * sum(size - 1 for size in levels)
    scratch = recv + part + [pltpu.SemaphoreType.DMA((slots,)), pltpu.SemaphoreType.DMA((slots,))]
    operands = [x]
    if small is not None:
        operands.append(small)
        scratch += [pltpu.VMEM((size,) + small.shape, small.dtype) for size in levels]
    return pl.pallas_call(
        functools.partial(sum_kernel, levels, chunks, small is not None),
        out_shape=[jax.ShapeDtypeStruct(a.shape, a.dtype) for a in operands],
        in_specs=[pl.BlockSpec(memory_space=pltpu.VMEM) for a in operands],
        out_specs=[pl.BlockSpec(memory_space=pltpu.VMEM) for a in operands],
        scratch_shapes=scratch,
        compiler_params=pltpu.CompilerParams(collective_id=ident, has_side_effects=True),
        name=f"sum_over_ga_{ident}",
    )(*operands)


def margins(occupied, vectors):
    turned = jnp.stack([vectors[:, 1], -vectors[:, 0]], axis=1)
    both = jnp.concatenate([vectors, turned], axis=2)
    return jnp.einsum("phmg,hng->pmn", both, occupied, precision=HIGH)


def correction(summed, occ_rows):
    half = summed.shape[1] // 2
    turned = jnp.concatenate([-summed[:, half:], summed[:, :half]], axis=1)
    coefficient = jnp.stack([summed, turned], axis=1)
    out = jnp.einsum("phmn,hng->pmg", coefficient, occ_rows, precision=HIGH)
    return out.reshape(out.shape[0], 2, half, out.shape[2])


def on_device(count, occupied, residual, old_direction, kin_ratio, old_dot):
    pert, _, bands, _ = residual.shape
    occ = occupied.shape[1]
    factor = teter_factor(kin_ratio)

    shape = (pert, 2 * bands, occ)
    lanes = occ if pert * 2 * bands % (8 * count) == 0 else 128

    def to_rows(s):
        return s.reshape(-1, lanes)

    def from_rows(r):
        return r.reshape(shape)

    first = from_rows(sum_over_ga(to_rows(margins(occupied, residual)), count, 0)[0])
    gradient = residual - correction(first, occupied)
    precond = factor * gradient
    local_dot = jnp.sum(factor * (gradient[:, 0] ** 2 + gradient[:, 1] ** 2), axis=-1)
    padded = jnp.pad(local_dot, ((0, -pert % 8), (0, 0)))
    second, dots = sum_over_ga(to_rows(margins(occupied, precond)), count, 1, padded)
    second = from_rows(second)
    dot_new = dots[:pert]
    projected = precond - correction(second, occupied)
    direction = projected + (dot_new / old_dot)[:, None, :, None] * old_direction
    return (direction, dot_new)


def solution(mesh):
    placed = (
        P(None, None, "ga"),
        P("groups", None, None, "ga"),
        P("groups", None, None, "ga"),
        P("ga"),
        P("groups", None),
    )
    return jax.shard_map(
        functools.partial(on_device, mesh.shape["ga"]),
        mesh=mesh,
        in_specs=placed,
        out_specs=(P("groups", None, None, "ga"), P("groups", None)),
        check_vma=False,
    )
```

time: 279 us -> 138 us (0.49)
  waiting for transfers between devices: 167 us -> 0 us
  Pallas kernels: 0 us -> 93.4 us
  blocking collectives: 31.1 us -> 0 us
  matrix products: 55.9 us -> 29.2 us
  between operations: 14.2 us -> 0.81 us
    psum x2 -> x0, waiting for transfers between devices: 167 us -> none  [the longest x1 100 us: on_device(): first_total = lax.psum(first, 'ga')]
    pallas_call x0 -> x2, Pallas kernels: none -> 93.4 us  [sum_over_ga(): pl.pallas_call(functools.partial(sum_kernel, levels, chunks, small is not...]
    psum x1 -> x0, blocking collectives: 31.1 us -> none  [on_device(): second_total, dot_new = lax.psum((second, local_dot), 'ga')]
    dot_general x4, matrix products: 55.9 us -> 29.2 us  [the longest x2 14.7 us: margins(): return jnp.einsum('phmg,hng->pmn', both, occupied, precision=HIGH)]
    another operation x4 -> x2, other arithmetic: 3.89 us -> 0.32 us  [correction(): coefficient = jnp.stack([summed, turned], axis=1)]
  transfers between devices with their start and end apart: 2 -> 0, of which waited for: 2 -> 0; matrix products, arithmetic and copies ran while one was open for 0% -> 0% of each run, Pallas kernels for 0% -> 0%
where the time goes in v1:
time: 138 us; the launch traced here: 137 us
  Pallas kernels  93.4 us (68%)
  matrix products  29.2 us (21%)
  other arithmetic  9.4 us (7%)
  local copies, waits for them, and re-layouts  3.91 us (3%)
    pallas_call x2, Pallas kernels, sum_over_ga(): pl.pallas_call(functools.partial(sum_kernel, levels, chunks, small is not...  93.4 us
    dot_general x2, matrix products, margins(): return jnp.einsum('phmg,hng->pmn', both, occupied, precision=HIGH)  14.7 us
    dot_general x2, matrix products, correction(): out = jnp.einsum('phmn,hng->pmg', coefficient, occ_rows, precision=HIGH)  14.5 us
    neg x2, other arithmetic, correction(): turned = jnp.concatenate([-summed[:, half:], summed[:, :half]], axis=1)  3.54 us
    unnamed x20, local copies, waits for them, and re-layouts  3.13 us

profile of v1, /device:TPU:0, one launch (start us, length us, event | category | flops | bytes accessed | tf_op | source)
XLA Modules:
  0.0 136.7 jit_solution(17853749451377000492)
XLA Ops:
  0.6 0.0 copy-start.3
  0.6 0.8 add_divide_fusion
  1.5 1.5 %fusion.38 = (f32[2,1,128,768]{3,2,1,0:T(8,128)S(1)}, f32[2,1,128,768]{3,2,1,0:T(8,128)S(1)}) fusion(f32[2,2,128,768]{3,2,1,0:T(8,128)} %param.6), kind=kLoop, calls=%fused_computation.52 | loop fusion | flops 196608 | bytes 3145728 | tf_op jit(solution)/shard_map/slice | solution.py:173
  3.0 8.2 %fusion.6 = f32[2,256,1024,1]{2,1,3,0:T(8,128)} fusion(f32[2,1024,768]{2,1,0:T(8,128)} %param.5, f32[2,1,128,768]{3,2,1,0:T(8,128)S(1)} %get-tuple-element.17, f32[2,1,128,768]{3,2,1,0:T(8,128)S(1)} %get-tuple-element.16, f32[2,2,128,768]{3,2,1,0:T(8,128)S(1)} %copy-done.3), kind=kOutput, calls=%fused_computation.6 | convolution fusion | flops 4833411072 | bytes 11534336 | tf_op jit(solution)/shard_map/phmg,hng->pmn/dot_general | solution.py:175
  11.2 48.8 %sum_over_ga_0.1 = f32[512,1024]{1,0:T(8,128)} custom-call(f32[512,1024]{1,0:T(8,128)} %bitcast.50), custom_call_target="tpu_custom_call" | custom-call | tf_op jit(solution)/shard_map/sum_over_ga_0/pallas_call | solution.py:161
  60.0 0.0 slice-start.1
  60.0 1.8 %slice_negate_fusion.1 = (f32[2,128,1024]{2,1,0:T(8,128)S(1)}, f32[2,128,1024]{2,1,0:T(8,128)S(1)}) fusion(f32[2,256,1024]{2,1,0:T(8,128)} %bitcast.45), kind=kLoop, calls=%fused_computation.28 | loop fusion | flops 262144 | bytes 4194304 | tf_op jit(solution)/shard_map/neg | solution.py:180
  61.8 0.2 maximum_bitcast_fusion
  62.0 0.8 slice-done.1
  62.8 0.9 copy-done.2
  63.7 5.5 %fusion.4 = f32[2,256,768,1]{2,1,3,0:T(8,128)S(1)} fusion(f32[2,1024,768]{2,1,0:T(8,128)S(1)} %bitcast.44, f32[2,1,256,1024]{3,2,1,0:T(8,128)S(1)} %maximum_bitcast_fusion, f32[2,1,256,1024]{3,2,1,0:T(8,128)S(1)} %bitcast.46), kind=kOutput, calls=%fused_computation.4 | convolution fusion | flops 4832886784 | bytes 12058624 | tf_op jit(solution)/shard_map/phmn,hng->pmg/dot_general | solution.py:182
  69.2 0.2 broadcast_multiply_fusion
  69.4 0.2 fusion.27
  69.6 0.8 pad.4.refs_1_
  70.4 0.1 fusion.37
  70.5 0.0 copy-done
  70.5 6.5 %fusion.2 = f32[2,256,1024,1]{2,1,3,0:T(8,128)} fusion(f32[2,1024,768]{2,1,0:T(8,128)S(1)} %bitcast.44, f32[2,1,128,768]{3,2,1,0:T(8,128)S(1)} %get-tuple-element.15, f32[2,1,128,768]{3,2,1,0:T(8,128)S(1)} %get-tuple-element.14, f32[2,2,128,768]{3,2,1,0:T(8,128)S(1)} %get-tuple-element.8), kind=kOutput, calls=%fused_computation.2 | convolution fusion | flops 4833411072 | bytes 11534336 | tf_op jit(solution)/shard_map/phmg,hng->pmn/dot_general | solution.py:175
  77.0 44.6 %sum_over_ga_1.1 = (f32[512,1024]{1,0:T(8,128)}, f32[8,128]{1,0:T(8,128)}) custom-call(f32[512,1024]{1,0:T(8,128)} %bitcast.49, f32[8,128]{1,0:T(8,128)} %pad.4.refs_1_), custom_call_target="tpu_custom_call" | custom-call | tf_op jit(solution)/shard_map/sum_over_ga_1/pallas_call | solution.py:161
  121.6 1.2 fusion.36
  122.9 1.7 %slice_negate_fusion = (f32[2,128,1024]{2,1,0:T(8,128)S(1)}, f32[2,128,1024]{2,1,0:T(8,128)S(1)}) fusion(f32[2,256,1024]{2,1,0:T(8,128)} %bitcast.47), kind=kLoop, calls=%fused_computation.27 | loop fusion | flops 262144 | bytes 4194304 | tf_op jit(solution)/shard_map/neg | solution.py:180
  124.6 0.1 maximum_bitcast_fusion.1
  124.7 1.4 %copy-done.5 = f32[512,1024]{1,0:T(8,128)S(1)} copy-done((f32[512,1024]{1,0:T(8,128)S(1)}, f32[512,1024]{1,0:T(8,128)}, u32[]{:S(2)}) %copy-start.5) | copy-done | bytes 2097176
  126.2 9.1 %fusion = f32[2,256,768,1]{2,1,3,0:T(8,128)S(1)} fusion(f32[2,1024,768]{2,1,0:T(8,128)} %param.5, f32[2,1,256,1024]{3,2,1,0:T(8,128)S(1)} %maximum_bitcast_fusion.1, f32[2,1,256,1024]{3,2,1,0:T(8,128)S(1)} %bitcast.48), kind=kOutput, calls=%fused_computation | convolution fusion | flops 4832886784 | bytes 12058624 | tf_op jit(solution)/shard_map/phmn,hng->pmg/dot_general | solution.py:182
  135.3 1.4 %multiply_add_fusion = f32[2,2,128,768]{3,2,1,0:T(8,128)} fusion(f32[2,2,128,768]{3,2,1,0:T(8,128)S(1)} %copy-done.6, f32[2,2,128,768]{3,2,1,0:T(8,128)S(1)} %copy-done.1, f32[2,2,128,768]{3,2,1,0:T(8,128)S(1)} %bitcast.52, f32[2,128]{1,0:T(2,128)S(1)} %get-tuple-element.6), kind=kLoop, calls=%fused_computation.26 | loop fusion | flops 1179648 | bytes 6292480 | tf_op jit(solution)/shard_map/add | solution.py:209
  (15 shorter events, 0.0 us)
Async XLA Ops:
  0.6 2.3 %copy-start.3 = (f32[2,2,128,768]{3,2,1,0:T(8,128)S(1)}, f32[2,2,128,768]{3,2,1,0:T(8,128)}, u32[]{:S(2)}) copy-start(f32[2,2,128,768]{3,2,1,0:T(8,128)} %param.6) | copy-start | bytes 4718596
  11.2 50.8 %slice-start = ((s8[6291456]{0:T(1024)(128)(4,1)}), s8[2097152]{0:T(1024)(128)(4,1)S(1)}, s32[]{:S(2)}) async-start(s8[6291456]{0:T(1024)(128)(4,1)} %bitcast.43), calls=%async_computation | async-start | bytes 4194304
  60.0 2.8 %slice-start.1 = ((s8[6291456]{0:T(1024)(128)(4,1)}), s8[4194304]{0:T(1024)(128)(4,1)S(1)}, s32[]{:S(2)}) async-start(s8[6291456]{0:T(1024)(128)(4,1)} %bitcast.43), calls=%async_computation.1 | async-start | bytes 8388608
  61.8 1.9 %copy-start.2 = (f32[512,1024]{1,0:T(8,128)S(1)}, f32[512,1024]{1,0:T(8,128)}, u32[]{:S(2)}) copy-start(f32[512,1024]{1,0:T(8,128)} %sum_over_ga_0.1) | copy-start | bytes 6291460
  63.7 5.5 %copy-start.4 = (f32[2,2,128,768]{3,2,1,0:T(8,128)S(1)}, f32[2,2,128,768]{3,2,1,0:T(8,128)}, u32[]{:S(2)}) copy-start(f32[2,2,128,768]{3,2,1,0:T(8,128)} %param.6) | copy-start | bytes 4718596
  69.4 1.1 copy-start
  77.0 44.6 %copy-start.7 = (f32[2,128]{1,0:T(2,128)S(1)}, f32[2,128]{1,0:T(2,128)}, u32[]{:S(2)}) copy-start(f32[2,128]{1,0:T(2,128)} %param.9) | copy-start | bytes 3076
  124.6 1.6 %copy-start.5 = (f32[512,1024]{1,0:T(8,128)S(1)}, f32[512,1024]{1,0:T(8,128)}, u32[]{:S(2)}) copy-start(f32[512,1024]{1,0:T(8,128)} %get-tuple-element.4) | copy-start | bytes 6291460
  126.2 9.1 %copy-start.1 = (f32[2,2,128,768]{3,2,1,0:T(8,128)S(1)}, f32[2,2,128,768]{3,2,1,0:T(8,128)}, u32[]{:S(2)}) copy-start(f32[2,2,128,768]{3,2,1,0:T(8,128)} %copy-done) | copy-start | bytes 4718596
  126.2 9.1 %copy-start.6 = (f32[2,2,128,768]{3,2,1,0:T(8,128)S(1)}, f32[2,2,128,768]{3,2,1,0:T(8,128)}, u32[]{:S(2)}) copy-start(f32[2,2,128,768]{3,2,1,0:T(8,128)} %param.7) | copy-start | bytes 4718596

commit v2 on v1

v2 whole, which is shorter than its diff:
```python
import functools
import math

import jax
import jax.numpy as jnp
from jax import lax
from jax.experimental import pallas as pl
from jax.experimental.pallas import tpu as pltpu
from jax.sharding import PartitionSpec as P


def teter_factor(ratio):
    numerator = 27.0 + 18.0 * ratio + 12.0 * ratio**2 + 8.0 * ratio**3
    return numerator / (numerator + 16.0 * ratio**4)


def levels_of(count):
    chips = count // 2
    inner = 2 ** (int(math.log2(chips)) // 2)
    return (2, inner, chips // inner)


def plan_of(levels, rows, lanes):
    cuts = []
    for size in levels:
        if rows % (8 * size) == 0:
            rows //= size
            cuts.append((0, rows, lanes))
        elif lanes % (128 * size) == 0:
            lanes //= size
            cuts.append((1, rows, lanes))
        else:
            return None
    return cuts


def split(x):
    high = x.astype(jnp.bfloat16)
    return high, (x - high.astype(jnp.float32)).astype(jnp.bfloat16)


def three_pass(a, b, dims):
    def dot(u, v):
        return lax.dot_general(u, v, (dims, ((), ())), preferred_element_type=jnp.float32)

    return dot(a[0], b[0]) + (dot(a[0], b[1]) + dot(a[1], b[0]))


def project_kernel(levels, cuts, pieces, small, *refs):
    depth = len(levels)
    if small:
        r_ref, occ_ref, d_ref, c_ref, e_ref, *scratch = refs
        gathered = scratch[-depth:]
        scratch = scratch[:-depth]
    else:
        r_ref, occ_ref, c_ref, *scratch = refs
    local, total, occ_high, occ_low, r_high, r_low, *scratch = scratch
    recv = scratch[:depth]
    part = scratch[depth : 2 * depth - 1]
    send_sem, recv_sem = scratch[2 * depth - 1 :]
    pert, rows, _ = r_ref.shape
    half = rows // 2
    width = occ_ref.shape[1] // pieces
    chunks = pert * pieces
    me = lax.axis_index("ga")
    coords, strides, stride = [], [], 1
    for size in levels:
        coords.append((me // stride) % size)
        strides.append(stride)
        stride *= size

    def peer(level, d):
        there = (coords[level] + d) % levels[level]
        return there, me + (there - coords[level]) * strides[level]

    barrier = pltpu.get_barrier_semaphore()
    count = 0
    for level in range(depth):
        for d in range(1, levels[level]):
            pl.semaphore_signal(barrier, inc=1, device_id={"ga": peer(level, d)[1]}, device_id_type=pl.DeviceIdType.MESH)
            count += 1

    copies = {}

    def send(chunk, stage, d, src, dst, device):
        slot = len(copies)
        copy = pltpu.make_async_remote_copy(
            src_ref=src,
            dst_ref=dst,
            send_sem=send_sem.at[slot],
            recv_sem=recv_sem.at[slot],
            device_id={"ga": device},
            device_id_type=pl.DeviceIdType.MESH,
        )
        copy.start()
        copies[(chunk, stage, d)] = copy

    def band(chunk):
        p, q = divmod(chunk, pieces)
        return p, q * width

    def inside(level, which, row, lane):
        axis, height, span = cuts[level]
        if axis == 0:
            return row + which * height, lane
        return row, lane + which * span

    def window(chunk, level, row, lane):
        _, height, span = cuts[level]
        return pl.ds(pl.multiple_of(row, 8), height), pl.ds(pl.multiple_of(lane, 128), span)

    def owned(chunk, level):
        p, lane = band(chunk)
        row = 0
        for k in range(level + 1):
            row, lane = inside(k, coords[k], row, lane)
        return total.at[(p,) + window(chunk, level, row, lane)]

    def source(chunk, level, which):
        if level == 0:
            p, lane = band(chunk)
            return local.at[(p,) + window(chunk, 0, *inside(0, which, 0, lane))]
        return part[level - 1].at[(chunk,) + window(chunk, level, *inside(level, which, 0, 0))]

    def form(chunk):
        p, lane = band(chunk)
        bands = pl.ds(lane, width)
        if p == 0:
            for h in range(2):
                occ_high[h, bands], occ_low[h, bands] = split(occ_ref[h, bands])
        if lane == 0:
            r_high[p], r_low[p] = split(r_ref[p])
        vectors = (r_high[p], r_low[p])
        first, second = (three_pass(vectors, (occ_high[h, bands], occ_low[h, bands]), ((1,), (1,))) for h in range(2))
        local[p, :half, bands] = first[:half] + second[half:]
        local[p, half:, bands] = first[half:] - second[:half]

    def correct(chunk):
        p, lane = band(chunk)
        bands = pl.ds(lane, width)
        summed = split(total[p, :, bands])
        first, second = (three_pass(summed, (occ_high[h, bands], occ_low[h, bands]), ((1,), (0,))) for h in range(2))
        upper = first[:half] - second[half:]
        lower = first[half:] + second[:half]
        if lane == 0:
            c_ref[p, :half] = upper
            c_ref[p, half:] = lower
        else:
            c_ref[p, :half] += upper
            c_ref[p, half:] += lower

    def stage_run(chunk, stage):
        if 1 <= stage <= depth:
            level = stage - 1
            value = source(chunk, level, coords[level])[...]
            for d in range(1, levels[level]):
                copies[(chunk, stage - 1, d)].wait_recv()
                value = value + recv[level][chunk, d - 1]
            if level < depth - 1:
                part[level][chunk] = value
            else:
                owned(chunk, depth - 1)[...] = value
        elif stage > depth:
            level = 2 * depth - stage
            for d in range(1, levels[level]):
                copies[(chunk, stage - 1, d)].wait_recv()
        if stage < depth:
            for d in range(1, levels[stage]):
                there, device = peer(stage, d)
                send(chunk, stage, d, source(chunk, stage, there), recv[stage].at[chunk, d - 1], device)
        elif stage < 2 * depth:
            level = 2 * depth - 1 - stage
            block = owned(chunk, level)
            for d in range(1, levels[level]):
                send(chunk, stage, d, block, block, peer(level, d)[1])
        else:
            correct(chunk)

    def small_run(stage):
        if stage == 0:
            value = d_ref[...]
        else:
            for d in range(1, levels[stage - 1]):
                copies[("small", stage - 1, d)].wait_recv()
            value = gathered[stage - 1][0]
            for k in range(1, levels[stage - 1]):
                value = value + gathered[stage - 1][k]
        if stage == depth:
            e_ref[...] = value
            return
        gathered[stage][coords[stage]] = value
        block = gathered[stage].at[coords[stage]]
        for d in range(1, levels[stage]):
            send("small", stage, d, block, block, peer(stage, d)[1])

    order = [0] + list(reversed(range(1, 2 * depth))) + [2 * depth]
    for turn in range(chunks + 2 * depth):
        for stage in order:
            chunk = turn - stage
            if 0 <= chunk < chunks:
                if stage == 0:
                    form(chunk)
                    if chunk == 0:
                        pl.semaphore_wait(barrier, count)
                stage_run(chunk, stage)
        if small and turn <= depth:
            small_run(turn)
    for copy in copies.values():
        copy.wait_send()


def project(vectors, occupied, count, ident, small=None):
    levels = levels_of(count)
    pert, rows, planes = vectors.shape
    occ = occupied.shape[1]
    for pieces in (4, 2, 1):
        cuts = plan_of(levels, rows, occ // pieces)
        if cuts is not None:
            break
    chunks = pert * pieces
    recv, part = [], []
    for level, size in enumerate(levels):
        shape = cuts[level][1:]
        recv.append(pltpu.VMEM((chunks, size - 1) + shape, jnp.float32))
        if level < len(levels) - 1:
            part.append(pltpu.VMEM((chunks,) + shape, jnp.float32))
    slots = (2 * chunks + 1) * sum(size - 1 for size in levels)
    scratch = [pltpu.VMEM((pert, rows, occ), jnp.float32)] * 2
    scratch += [pltpu.VMEM(occupied.shape, jnp.bfloat16)] * 2 + [pltpu.VMEM(vectors.shape, jnp.bfloat16)] * 2
    scratch += recv + part + [pltpu.SemaphoreType.DMA((slots,)), pltpu.SemaphoreType.DMA((slots,))]
    operands = [vectors, occupied]
    outs = [jax.ShapeDtypeStruct(vectors.shape, vectors.dtype)]
    if small is not None:
        operands.append(small)
        outs.append(jax.ShapeDtypeStruct(small.shape, small.dtype))
        scratch += [pltpu.VMEM((size,) + small.shape, small.dtype) for size in levels]
    return pl.pallas_call(
        functools.partial(project_kernel, levels, cuts, pieces, small is not None),
        out_shape=outs,
        in_specs=[pl.BlockSpec(memory_space=pltpu.VMEM) for _ in operands],
        out_specs=[pl.BlockSpec(memory_space=pltpu.VMEM) for _ in outs],
        scratch_shapes=scratch,
        compiler_params=pltpu.CompilerParams(collective_id=ident, has_side_effects=True),
        name=f"project_{ident}",
    )(*operands)


def on_device(count, occupied, residual, old_direction, kin_ratio, old_dot):
    pert, _, bands, planes = residual.shape
    flat = (pert, 2 * bands, planes)
    factor = teter_factor(kin_ratio)
    (first,) = project(residual.reshape(flat), occupied, count, 0)
    gradient = residual - first.reshape(residual.shape)
    precond = factor * gradient
    local_dot = jnp.sum(factor * (gradient[:, 0] ** 2 + gradient[:, 1] ** 2), axis=-1)
    padded = jnp.pad(local_dot, ((0, -pert % 8), (0, 0)))
    second, dots = project(precond.reshape(flat), occupied, count, 1, padded)
    dot_new = dots[:pert]
    projected = precond - second.reshape(residual.shape)
    direction = projected + (dot_new / old_dot)[:, None, :, None] * old_direction
    return (direction, dot_new)


def solution(mesh):
    placed = (
        P(None, None, "ga"),
        P("groups", None, None, "ga"),
        P("groups", None, None, "ga"),
        P("ga"),
        P("groups", None),
    )
    return jax.shard_map(
        functools.partial(on_device, mesh.shape["ga"]),
        mesh=mesh,
        in_specs=placed,
        out_specs=(P("groups", None, None, "ga"), P("groups", None)),
        check_vma=False,
    )
```

time: 138 us -> 131 us (0.949)
  matrix products: 29.2 us -> 0 us
  Pallas kernels: 93.4 us -> 122 us
  local copies, waits for them, and re-layouts: 3.91 us -> 0.62 us
  other arithmetic: 9.4 us -> 7.8 us
    dot_general x4 -> x0, matrix products: 29.2 us -> none  [the longest x2 14.7 us: margins(): return jnp.einsum('phmg,hng->pmn', both, occupied, precision=HIGH)]
    pallas_call x2, Pallas kernels: 93.4 us -> 122 us  [project(): pl.pallas_call(functools.partial(project_kernel, levels, cuts, pieces, sm...]
    neg x2 -> x0, other arithmetic: 3.54 us -> none  [correction(): turned = jnp.concatenate([-summed[:, half:], summed[:, :half]], axis=1)]
    unnamed x20 -> x8, local copies, waits for them, and re-layouts: 3.13 us -> 0.01 us
    mul x1, other arithmetic: 0.21 us -> 2.83 us  [on_device(): precond = factor * gradient]
    slice x2 -> x0, other arithmetic: 1.62 us -> none  [margins(): turned = jnp.stack([vectors[:, 1], -vectors[:, 0]], axis=1)]
where the time goes in v2:
time: 131 us
  Pallas kernels  122 us (93%)
  other arithmetic  7.8 us (6%)
    pallas_call x2, Pallas kernels, project(): pl.pallas_call(functools.partial(project_kernel, levels, cuts, pieces, sm...  122 us
    mul x1, other arithmetic, on_device(): precond = factor * gradient  2.83 us
    add x1, other arithmetic, on_device(): projected + (dot_new / old_dot)[:, None, :, None] * old_direction  2.82 us

profile of v2, /device:TPU:0, one launch (start us, length us, event | category | flops | bytes accessed | tf_op | source)
XLA Modules:
  0.0 131.0 jit_solution(7422688491780563533)
XLA Ops:
  0.6 0.7 add_divide_fusion
  1.3 0.0 copy-start.1
  1.3 63.1 %project_0.1 = f32[2,256,768]{2,1,0:T(8,128)} custom-call(f32[2,256,768]{2,1,0:T(8,128)} %bitcast.11, f32[2,1024,768]{2,1,0:T(8,128)} %refs_1_.3), custom_call_target="tpu_custom_call" | custom-call | tf_op jit(solution)/shard_map/project_0/pallas_call | solution.py:237
  64.5 0.0 copy-done.1
  64.5 2.8 %broadcast_multiply_fusion = (f32[2,2,128,768]{3,2,1,0:T(8,128)}, f32[2,2,128,768]{3,2,1,0:T(8,128)S(1)}) fusion(f32[768]{0:T(1024)S(1)} %add_divide_fusion, f32[2,2,128,768]{3,2,1,0:T(8,128)S(1)} %copy-done.1, f32[2,2,128,768]{3,2,1,0:T(8,128)} %bitcast.12), kind=kLoop, calls=%fused_computation.7 | loop fusion | flops 786432 | bytes 6294528 | tf_op jit(solution)/shard_map/mul | solution.py:254
  67.3 0.2 fusion.3
  67.5 0.6 pad.4.refs_2_
  68.1 0.0 copy-start.3
  68.1 0.0 copy-start
  68.1 0.0 copy-start.2
  68.1 58.8 %project_1.1 = (f32[2,256,768]{2,1,0:T(8,128)}, f32[8,128]{1,0:T(8,128)}) custom-call(f32[2,256,768]{2,1,0:T(8,128)} %bitcast.10, f32[2,1024,768]{2,1,0:T(8,128)} %refs_1_.3, f32[8,128]{1,0:T(8,128)} %pad.4.refs_2_), custom_call_target="tpu_custom_call" | custom-call | tf_op jit(solution)/shard_map/project_1/pallas_call | solution.py:237
  126.9 0.0 copy-done.3
  126.9 1.2 fusion.8
  128.2 0.0 copy-done
  128.2 0.0 copy-done.2
  128.2 2.8 %multiply_add_fusion = f32[2,2,128,768]{3,2,1,0:T(8,128)} fusion(f32[2,2,128,768]{3,2,1,0:T(8,128)S(1)} %copy-done.2, f32[2,2,128,768]{3,2,1,0:T(8,128)S(1)} %copy-done, f32[2,2,128,768]{3,2,1,0:T(8,128)} %bitcast.13, f32[2,128]{1,0:T(2,128)S(1)} %get-tuple-element.6), kind=kLoop, calls=%fused_computation | loop fusion | flops 1179648 | bytes 6292480 | tf_op jit(solution)/shard_map/add | solution.py:260
Async XLA Ops:
  1.3 63.2 %copy-start.1 = (f32[2,2,128,768]{3,2,1,0:T(8,128)S(1)}, f32[2,2,128,768]{3,2,1,0:T(8,128)}, u32[]{:S(2)}) copy-start(f32[2,2,128,768]{3,2,1,0:T(8,128)} %param.6) | copy-start | bytes 4718596
  68.1 58.8 %copy-start.3 = (f32[2,128]{1,0:T(2,128)S(1)}, f32[2,128]{1,0:T(2,128)}, u32[]{:S(2)}) copy-start(f32[2,128]{1,0:T(2,128)} %param.9) | copy-start | bytes 3076
  68.1 60.0 %copy-start = (f32[2,2,128,768]{3,2,1,0:T(8,128)S(1)}, f32[2,2,128,768]{3,2,1,0:T(8,128)}, u32[]{:S(2)}) copy-start(f32[2,2,128,768]{3,2,1,0:T(8,128)} %get-tuple-element.8) | copy-start | bytes 4718596
  68.1 60.0 %copy-start.2 = (f32[2,2,128,768]{3,2,1,0:T(8,128)S(1)}, f32[2,2,128,768]{3,2,1,0:T(8,128)}, u32[]{:S(2)}) copy-start(f32[2,2,128,768]{3,2,1,0:T(8,128)} %param.7) | copy-start | bytes 4718596

commit v3 on v2

--- a/solution.py
+++ b/solution.py
@@ -213,7 +213,7 @@
     levels = levels_of(count)
     pert, rows, planes = vectors.shape
     occ = occupied.shape[1]
-    for pieces in (4, 2, 1):
+    for pieces in (2, 1):
         cuts = plan_of(levels, rows, occ // pieces)
         if cuts is not None:
             break

time: 131 us -> 120 us (0.916)
  Pallas kernels: 122 us -> 110 us
    pallas_call x2, Pallas kernels: 122 us -> 110 us  [project(): pl.pallas_call(functools.partial(project_kernel, levels, cuts, pieces, sm...]
where the time goes in v3:
time: 120 us
  Pallas kernels  110 us (92%)
  other arithmetic  7.8 us (6%)
    pallas_call x2, Pallas kernels, project(): pl.pallas_call(functools.partial(project_kernel, levels, cuts, pieces, sm...  110 us
    mul x1, other arithmetic, on_device(): precond = factor * gradient  2.83 us
    add x1, other arithmetic, on_device(): projected + (dot_new / old_dot)[:, None, :, None] * old_direction  2.82 us

profile of v3, /device:TPU:0, one launch (start us, length us, event | category | flops | bytes accessed | tf_op | source)
XLA Modules:
  0.0 119.5 jit_solution(10145722097685680158)
XLA Ops:
  0.6 0.7 add_divide_fusion
  1.3 0.0 copy-start.1
  1.3 55.7 %project_0.1 = f32[2,256,768]{2,1,0:T(8,128)} custom-call(f32[2,256,768]{2,1,0:T(8,128)} %bitcast.11, f32[2,1024,768]{2,1,0:T(8,128)} %refs_1_.3), custom_call_target="tpu_custom_call" | custom-call | tf_op jit(solution)/shard_map/project_0/pallas_call | solution.py:237
  57.1 0.0 copy-done.1
  57.1 2.8 %broadcast_multiply_fusion = (f32[2,2,128,768]{3,2,1,0:T(8,128)}, f32[2,2,128,768]{3,2,1,0:T(8,128)S(1)}) fusion(f32[768]{0:T(1024)S(1)} %add_divide_fusion, f32[2,2,128,768]{3,2,1,0:T(8,128)S(1)} %copy-done.1, f32[2,2,128,768]{3,2,1,0:T(8,128)} %bitcast.12), kind=kLoop, calls=%fused_computation.7 | loop fusion | flops 786432 | bytes 6294528 | tf_op jit(solution)/shard_map/mul | solution.py:254
  59.9 0.2 fusion.3
  60.1 0.6 pad.4.refs_2_
  60.7 0.0 copy-start.3
  60.7 0.0 copy-start
  60.7 0.0 copy-start.2
  60.7 54.7 %project_1.1 = (f32[2,256,768]{2,1,0:T(8,128)}, f32[8,128]{1,0:T(8,128)}) custom-call(f32[2,256,768]{2,1,0:T(8,128)} %bitcast.10, f32[2,1024,768]{2,1,0:T(8,128)} %refs_1_.3, f32[8,128]{1,0:T(8,128)} %pad.4.refs_2_), custom_call_target="tpu_custom_call" | custom-call | tf_op jit(solution)/shard_map/project_1/pallas_call | solution.py:237
  115.4 0.0 copy-done.3
  115.5 1.2 %fusion.8 = (f32[2,128]{1,0:T(2,128)S(1)}, f32[2,128]{1,0:T(2,128)}) fusion(f32[2,128]{1,0:T(2,128)S(1)} %copy-done.3, f32[8,128]{1,0:T(8,128)} %get-tuple-element.5), kind=kLoop, calls=%fused_computation.16 | loop fusion | flops 256 | bytes 4096 | tf_op jit(solution)/shard_map/div | solution.py:260
  116.7 0.0 copy-done
  116.7 0.0 copy-done.2
  116.7 2.8 %multiply_add_fusion = f32[2,2,128,768]{3,2,1,0:T(8,128)} fusion(f32[2,2,128,768]{3,2,1,0:T(8,128)S(1)} %copy-done.2, f32[2,2,128,768]{3,2,1,0:T(8,128)S(1)} %copy-done, f32[2,2,128,768]{3,2,1,0:T(8,128)} %bitcast.13, f32[2,128]{1,0:T(2,128)S(1)} %get-tuple-element.6), kind=kLoop, calls=%fused_computation | loop fusion | flops 1179648 | bytes 6292480 | tf_op jit(solution)/shard_map/add | solution.py:260
Async XLA Ops:
  1.3 55.8 %copy-start.1 = (f32[2,2,128,768]{3,2,1,0:T(8,128)S(1)}, f32[2,2,128,768]{3,2,1,0:T(8,128)}, u32[]{:S(2)}) copy-start(f32[2,2,128,768]{3,2,1,0:T(8,128)} %param.6) | copy-start | bytes 4718596
  60.7 54.7 %copy-start.3 = (f32[2,128]{1,0:T(2,128)S(1)}, f32[2,128]{1,0:T(2,128)}, u32[]{:S(2)}) copy-start(f32[2,128]{1,0:T(2,128)} %param.9) | copy-start | bytes 3076
  60.7 56.0 %copy-start = (f32[2,2,128,768]{3,2,1,0:T(8,128)S(1)}, f32[2,2,128,768]{3,2,1,0:T(8,128)}, u32[]{:S(2)}) copy-start(f32[2,2,128,768]{3,2,1,0:T(8,128)} %get-tuple-element.8) | copy-start | bytes 4718596
  60.7 56.0 %copy-start.2 = (f32[2,2,128,768]{3,2,1,0:T(8,128)S(1)}, f32[2,2,128,768]{3,2,1,0:T(8,128)}, u32[]{:S(2)}) copy-start(f32[2,2,128,768]{3,2,1,0:T(8,128)} %param.7) | copy-start | bytes 4718596
